TPU v7x, 32 devices: a whole 2x2x4 slice. The times are simulated.
32 devices in a mesh: dp: 16 (over z, y, core), space: 2 (over x).
Axes of the slice: x: 2, y: 2, z: 4, core: 2. Of those that a mesh axis runs over, the one named last changes fastest.
Arguments:
- images: bfloat16 [16, 3, 512, 512], P('dp', None, 'space'), may hold values from -6 to 6
- pos_embed: bfloat16 [1024, 1280], P('space'), may hold values from -3 to 3
- conv_first: bfloat16 [3, 3, 3, 64], replicated, may hold values from -1.75 to 1.75
- conv_second: bfloat16 [3, 3, 64, 128], replicated, may hold values from -0.375 to 0.375
- conv_third: bfloat16 [3, 3, 128, 256], replicated, may hold values from -0.25 to 0.25
- conv_fourth: bfloat16 [3, 3, 256, 512], replicated, may hold values from -0.1875 to 0.1875
- proj_weight: bfloat16 [512, 1280], replicated, may hold values from -0.375 to 0.375
- ln_first: float32 [1280], replicated, may hold values from 0.25 to 1.75
- qkv_weight: bfloat16 [1280, 3, 1280], P('dp', None, 'space'), as said below
- out_weight: bfloat16 [1280, 1280], P('space', 'dp'), may hold values from -0.15625 to 0.15625
- ln_second: float32 [1280], replicated, may hold values from 0.25 to 1.75
- up_weight: bfloat16 [1280, 5120], P('dp', 'space'), may hold values from -0.15625 to 0.15625
- down_weight: bfloat16 [5120, 1280], P('space', 'dp'), may hold values from -0.125 to 0.125
Outputs:
- encoded: bfloat16 [16, 1024, 1280], P('dp', 'space')
Inputs may be any that keep to these rules, and one draw needn't show every extreme that they name: `qkv_weight`: every entry is at most 135 * 1280 ** -0.5 in magnitude.
All inputs are finite; a program needn't handle non-finite values.
Results may differ from a plain program's by a relative error of at most 0.014.
Values may be sent and summed in bfloat16 or wider, within the bound.
A program may use at most 128 MiB of HBM per device.

v0:
```python
import jax
import jax.numpy as jnp
from jax import lax
from jax.sharding import PartitionSpec as P

HEADS = 16


def passed_along(value, axis, steps):
    count = lax.axis_size(axis)
    leading, last = (max(0, -steps), min(count, count - steps))
    return lax.ppermute(value, axis, [(source, source + steps) for source in range(leading, last)])


def conv_rows(image_field, kernel, spec):
    out = lax.conv_general_dilated(
        image_field,
        kernel,
        (2, 2),
        ((0, 0), (1, 1)),
        dimension_numbers=spec,
        preferred_element_type=jnp.float32,
    )
    return jax.nn.relu(out).astype(jnp.bfloat16)


def layer_norm(values, gain):
    wide = values.astype(jnp.float32)
    center = wide - jnp.mean(wide, axis=-1, keepdims=True)
    spread = jnp.mean(center * center, axis=-1, keepdims=True)
    return (center * lax.rsqrt(spread + 1e-06) * gain).astype(jnp.bfloat16)


def attend(query, keys, values):
    head_size = query.shape[-1]
    divisor = jnp.sqrt(jnp.float32(head_size))

    def one_head(items):
        head_query, head_keys, head_values = items
        scores = (
            jnp.einsum("gqd,gkd->gqk", head_query, head_keys, preferred_element_type=jnp.float32)
            / divisor
        )
        weights = jax.nn.softmax(scores, axis=-1).astype(jnp.bfloat16)
        return jnp.einsum(
            "gqk,gkd->gqd", weights, head_values, preferred_element_type=jnp.float32
        ).astype(jnp.bfloat16)

    mixed = lax.map(
        one_head, (jnp.moveaxis(query, 2, 0), jnp.moveaxis(keys, 2, 0), jnp.moveaxis(values, 2, 0))
    )
    return jnp.moveaxis(mixed, 0, 2)


def device_rows(values, start, total, groups, per_device, weight):
    token_start = start // groups
    token_count = total // groups
    slab = lax.dynamic_slice_in_dim(values, token_start, token_count, 1)
    owners = token_count // per_device
    slab = slab.reshape(groups, owners, per_device, values.shape[2])
    slab = jnp.transpose(slab, (1, 0, 2, 3)).reshape(total, values.shape[2])
    return jnp.dot(slab, weight, preferred_element_type=jnp.float32)


def on_device(
    images,
    pos_embed,
    conv_first,
    conv_second,
    conv_third,
    conv_fourth,
    proj_weight,
    ln_first,
    qkv_weight,
    out_weight,
    ln_second,
    up_weight,
    down_weight,
):
    spec_first = ("NCHW", "HWIO", "NHWC")
    spec_later = ("NHWC", "HWIO", "NHWC")
    margin = passed_along(images[:, :, -15:, :], "space", 1)
    stem_out = conv_rows(jnp.concatenate([margin, images], axis=2), conv_first, spec_first)
    for kernel in (conv_second, conv_third, conv_fourth):
        stem_out = conv_rows(stem_out, kernel, spec_later)
    groups, height, across, channels = stem_out.shape
    flat = stem_out.reshape(groups, height * across, channels)
    tokens = (
        jnp.dot(flat, proj_weight, preferred_element_type=jnp.float32)
        + pos_embed.astype(jnp.float32)
    ).astype(jnp.bfloat16)
    qkv_part, out_part = (
        lax.all_gather(qkv_weight, "dp", axis=0, tiled=True),
        lax.all_gather(out_weight, "dp", axis=1, tiled=True),
    )
    width = tokens.shape[2]
    count = tokens.shape[1]
    local = qkv_part.shape[2]
    head_size = width // HEADS
    local_heads = local // head_size
    qkv_matrix = qkv_part.reshape(width, 3 * local)
    qkv_all = jnp.dot(
        layer_norm(lax.all_gather(tokens, "space", axis=1, tiled=True), ln_first),
        qkv_matrix,
        preferred_element_type=jnp.float32,
    ).astype(jnp.bfloat16)
    seen = qkv_all.shape[1]
    qkv_all = qkv_all.reshape(groups, seen, 3, local_heads, head_size)
    mixed = attend(qkv_all[:, :, 0], qkv_all[:, :, 1], qkv_all[:, :, 2]).reshape(
        groups, seen, local
    )
    attn_sum = (
        lax.psum_scatter(
            device_rows(
                mixed,
                jnp.int32(0),
                groups * count * lax.axis_size("space"),
                groups,
                count,
                out_part,
            ).astype(jnp.bfloat16),
            "space",
            scatter_dimension=0,
            tiled=True,
        )
        .astype(jnp.float32)
        .reshape(groups, count, width)
    )
    after_attn = (tokens.astype(jnp.float32) + attn_sum).astype(jnp.bfloat16)
    normed_two = layer_norm(after_attn, ln_second)
    group_rows = lax.all_gather(normed_two, "space", axis=1, tiled=True)
    seen_rows = group_rows.shape[1]
    hidden_cols = up_weight.shape[1]
    start_hidden = jnp.zeros((groups, seen_rows, hidden_cols), jnp.float32)
    before_gelu = start_hidden + jnp.einsum(
        "gtd,df->gtf",
        group_rows,
        lax.all_gather(up_weight, "dp", axis=0, tiled=True),
        preferred_element_type=jnp.float32,
    )
    hidden = jax.nn.gelu(before_gelu, approximate=False).astype(jnp.bfloat16)
    down_part = lax.all_gather(down_weight, "dp", axis=1, tiled=True)
    mlp_sum = (
        lax.psum_scatter(
            device_rows(
                hidden,
                jnp.int32(0),
                groups * count * lax.axis_size("space"),
                groups,
                count,
                down_part,
            ).astype(jnp.bfloat16),
            "space",
            scatter_dimension=0,
            tiled=True,
        )
        .astype(jnp.float32)
        .reshape(groups, count, width)
    )
    return (after_attn.astype(jnp.float32) + mlp_sum).astype(jnp.bfloat16)


def solution(mesh):
    placed = (
        P("dp", None, "space", None),
        P("space", None),
        P(),
        P(),
        P(),
        P(),
        P(),
        P(),
        P("dp", None, "space"),
        P("space", "dp"),
        P(),
        P("dp", "space"),
        P("space", "dp"),
    )
    return jax.shard_map(
        on_device, mesh=mesh, in_specs=placed, out_specs=P("dp", "space", None), check_vma=False
    )
```

profile of v0, /device:TPU:0, one launch (start us, length us, event | category | flops | bytes accessed | tf_op | source)
XLA Modules:
  0.0 586.7 jit_solution(12435895969867735964)
XLA Ops:
  6.5 1.0 slice.12
  7.5 4.9 collective-permute-start
  12.4 1.7 collective-permute-done
  14.1 1.3 maximum_bitcast_fusion
  15.9 2.9 reshape.228
  18.8 19.6 %copy.46 = bf16[3,271,1,8,66]{3,0,4,1,2:T(4,128)(2,1)} copy(bf16[3,271,1,8,66]{4,3,1,0,2:T(8,128)(2,1)} %reshape.228) | data formatting | bytes 1717056 | tf_op jit(solution)/shard_map/conv_general_dilated | solution.py:16
  38.3 1.4 slice.25
  39.8 27.8 %fusion.44 = bf16[135,8,33,64]{3,1,2,0:T(8,128)(2,1)} fusion(pred[8,33]{0,1:T(8,128)(4,1)S(1)} %copy-done.8, bf16[3,3,3,64]{3,2,1,0:T(4,128)(2,1)S(1)} %copy-done.6, bf16[3,271,1,7,2]{3,0,4,1,2:T(4,128)(2,1)S(1)} %slice.25, bf16[3,271,1,8,66]{3,0,4,1,2:T(4,128)(2,1)} %copy.46), kind=kOutput, calls=%fused_computation.57 | convolution fusion | flops 134949312 | bytes 5446932 | tf_op jit(solution)/shard_map/conv_general_dilated | solution.py:16
  67.6 16.3 %copy.47 = bf16[135,8,33,64]{0,3,2,1:T(8,128)(2,1)} copy(bf16[135,8,33,64]{3,1,2,0:T(8,128)(2,1)} %fusion.44) | data formatting | bytes 9123840 | tf_op jit(solution)/shard_map/convert_element_type | solution.py:24
  84.0 8.3 %slice.26 = bf16[135,1,256,64]{0,3,2,1:T(8,128)(2,1)} slice(bf16[135,1,264,64]{0,3,2,1:T(8,128)(2,1)} %bitcast.122), slice={[0:135], [0:1], [0:256], [0:64]} | slice | bytes 8847360 | tf_op jit(solution)/shard_map/convert_element_type | solution.py:24
  92.3 15.6 %copy.48 = bf16[135,1,8,32,64]{4,2,3,0,1:T(8,128)(2,1)} copy(bf16[135,1,8,32,64]{0,4,3,2,1:T(8,128)(2,1)} %bitcast.123) | data formatting | bytes 8847360 | tf_op jit(solution)/shard_map/convert_element_type | solution.py:24
  107.9 1.1 fusion.155
  109.1 6.6 %fusion.86 = bf16[67,1,8,16,128]{4,2,3,0,1:T(8,128)(2,1)S(1)} fusion(bf16[3,3,64,128]{3,2,1,0:T(8,128)(2,1)S(1)} %copy-done.5, bf16[135,1,7,1,64]{4,2,3,0,1:T(8,128)(2,1)S(1)} %get-tuple-element.63, bf16[135,1,7,1,64]{4,2,3,0,1:T(8,128)(2,1)S(1)} %get-tuple-element.62, bf16[135,1,8,32,64]{4,2,3,0,1:T(8,128)(2,1)} %copy.48), kind=kOutput, calls=%fused_computation.105 | convolution fusion | flops 1290278912 | bytes 7008512 | tf_op jit(solution)/shard_map/conv_general_dilated | solution.py:16
  115.8 1.6 fusion.91
  117.5 1.4 fusion.105
  119.3 3.7 fusion.63
  123.0 0.7 all-gather.9.cloned.1.call-update
  123.8 0.7 all-gather.11.cloned.1.call-update
  124.5 39.7 %all-gather.17.cloned.1.call-done = bf16[1024,1280]{1,0:T(8,128)(2,1)} async-done(((bf16[512,1280]{1,0:T(8,128)(2,1)}), bf16[1024,1280]{1,0:T(8,128)(2,1)}) %all-gather.17.cloned.1.call-update) | async-done | bytes 2621456 | tf_op jit(solution)/shard_map/all_gather | solution.py:103
  164.2 2.1 convert_reduce_fusion
  166.4 2.6 fusion.50
  169.0 51.6 %all-gather.9.cloned.1.call-done = bf16[1280,3,640]{2,0,1:T(8,128)(2,1)} async-done(((bf16[80,3,640]{2,0,1:T(8,128)(2,1)}), bf16[1280,3,640]{2,0,1:T(8,128)(2,1)}) %all-gather.9.cloned.1.call-update) | async-done | bytes 4915216 | tf_op jit(solution)/shard_map/all_gather | solution.py:93
  220.6 8.2 %copy.52 = bf16[1280,3,640]{0,2,1:T(8,128)(2,1)} copy(bf16[1280,3,640]{2,0,1:T(8,128)(2,1)} %all-gather.9.cloned.1.call-done) | data formatting | bytes 9830400 | tf_op jit(solution)/shard_map/all_gather | solution.py:93
  228.8 10.3 %convolution_convert_fusion.1 = bf16[1024,1920]{1,0:T(8,128)(2,1)} fusion(bf16[1280,1920]{0,1:T(8,128)(2,1)} %bitcast.125, bf16[1024,1280]{1,0:T(8,128)(2,1)} %all-gather.17.cloned.1.call-done, f32[1280]{0:T(1024)S(1)} %copy-done.7, f32[1024]{0:T(1024)S(1)} %add_rsqrt_fusion, f32[1024]{0:T(1024)S(1)} %broadcast_multiply_fusion), kind=kOutput, calls=%fused_computation.78 | convolution fusion | flops 5041684480 | bytes 11482112 | tf_op jit(solution)/shard_map/dot_general | solution.py:102
  239.0 6.3 %copy.53 = bf16[1024,1920]{0,1:T(8,128)(2,1)} copy(bf16[1024,1920]{1,0:T(8,128)(2,1)} %convolution_convert_fusion.1) | data formatting | bytes 7864320 | tf_op jit(solution)/shard_map/convert_element_type | solution.py:106
  245.3 4.2 slice_bitcast_fusion
  249.5 39.8 %while.10 = (s32[]{:T(128)}, bf16[8,1,1024,80]{2,3,1,0:T(8,128)(2,1)}, bf16[8,1,1024,80]{2,3,0,1:T(8,128)(2,1)}, bf16[8,1,1024,80]{2,3,0,1:T(8,128)(2,1)S(1)}, bf16[8,1,1024,80]{2,3,0,1:T(8,128)(2,1)}, /*index=5*/s32[]{:T(128)}) while((s32[]{:T(128)}, bf16[8,1,1024,80]{2,3,1,0:T(8,128)(2,1)}, bf16[8,1,1024,80]{2,3,0,1:T(8,128)(2,1)}, ...), condition=%wide.region_5.6_spmd, body=%wide.region_2.5_spmd.sunk | while | flops 345061376 | bytes 13260869 | solution.py:49
  249.5 1.7 multiply_reduce_fusion.2
  251.2 0.7 fusion.186
  252.0 2.6 fusion.187
  254.5 1.7 multiply_reduce_fusion.2
  256.2 0.7 fusion.186
  256.9 2.6 fusion.187
  259.5 1.7 multiply_reduce_fusion.2
  261.2 0.7 fusion.186
  261.9 2.6 fusion.187
  264.5 1.7 multiply_reduce_fusion.2
  266.2 0.7 fusion.186
  266.9 2.6 fusion.187
  269.5 1.7 multiply_reduce_fusion.2
  271.1 0.7 fusion.186
  271.9 2.6 fusion.187
  274.4 1.7 multiply_reduce_fusion.2
  276.1 0.7 fusion.186
  276.9 2.6 fusion.187
  279.4 1.7 multiply_reduce_fusion.2
  281.1 0.7 fusion.186
  281.8 2.6 fusion.187
  284.4 1.7 multiply_reduce_fusion.2
  286.1 0.7 fusion.186
  286.8 2.6 fusion.187
  289.4 5.5 convolution_convert_fusion
  295.0 0.5 all-gather.13.cloned.1.call-update
  295.6 0.5 all-gather.15.cloned.1.call-update
  296.2 35.4 %reduce-scatter.3.cloned.1.call-done = bf16[512,1280]{1,0:T(8,128)(2,1)} async-done(((bf16[1024,1280]{1,0:T(8,128)(2,1)}), bf16[512,1280]{1,0:T(8,128)(2,1)}) %reduce-scatter.3.cloned.1.call-update) | async-done | bytes 1310736 | tf_op jit(solution)/shard_map/reduce_scatter | solution.py:113
  331.5 2.2 convert_reduce_fusion.1
  334.2 0.6 copy-done.2
  334.8 1.5 fusion.68
  336.4 60.2 %all-gather.13.cloned.1.call-done = bf16[1280,2560]{1,0:T(8,128)(2,1)} async-done(((bf16[80,2560]{1,0:T(8,128)(2,1)}), bf16[1280,2560]{1,0:T(8,128)(2,1)}) %all-gather.13.cloned.1.call-update) | async-done | bytes 6553616 | tf_op jit(solution)/shard_map/all_gather | solution.py:138
  396.6 63.7 %all-gather.15.cloned.1.call-done = bf16[2560,1280]{0,1:T(8,128)(2,1)} async-done(((bf16[2560,80]{0,1:T(8,128)(2,1)}), bf16[2560,1280]{0,1:T(8,128)(2,1)}) %all-gather.15.cloned.1.call-update) | async-done | bytes 6553616 | tf_op jit(solution)/shard_map/all_gather | solution.py:142
  460.3 39.3 %all-gather.19.cloned.1.call-done = bf16[1024,1280]{1,0:T(8,128)(2,1)} async-done(((bf16[512,1280]{1,0:T(8,128)(2,1)}), bf16[1024,1280]{1,0:T(8,128)(2,1)}) %all-gather.19.cloned.1.call-update) | async-done | bytes 2621456 | tf_op jit(solution)/shard_map/all_gather | solution.py:131
  499.6 38.9 %fusion.58 = bf16[1024,1280]{1,0:T(8,128)(2,1)} fusion(bf16[2560,1280]{0,1:T(8,128)(2,1)} %all-gather.15.cloned.1.call-done, bf16[1024,1280]{1,0:T(8,128)(2,1)} %all-gather.19.cloned.1.call-done, bf16[1280,2560]{1,0:T(8,128)(2,1)} %all-gather.13.cloned.1.call-done), kind=kOutput, calls=%fused_computation.76 | convolution fusion | flops 13593477120 | bytes 18350080 | tf_op jit(solution)/shard_map/dot_general | solution.py:62
  538.5 37.8 %reduce-scatter.5.cloned.1.call-done = bf16[512,1280]{1,0:T(8,128)(2,1)} async-done(((bf16[1024,1280]{1,0:T(8,128)(2,1)}), bf16[512,1280]{1,0:T(8,128)(2,1)}) %reduce-scatter.5.cloned.1.call-update) | async-done | bytes 1310736 | tf_op jit(solution)/shard_map/reduce_scatter | solution.py:144
  576.4 3.1 fusion.104
  (41 shorter events, 1.9 us)
Async XLA Ops:
  6.5 110.9 %copy-start = (bf16[3,3,256,512]{3,2,1,0:T(8,128)(2,1)S(1)}, bf16[3,3,256,512]{3,2,1,0:T(8,128)(2,1)}, u32[]{:S(2)}) copy-start(bf16[3,3,256,512]{3,2,1,0:T(8,128)(2,1)} %param.20) | copy-start | bytes 7077892
  6.5 157.7 %all-gather.17.cloned.1.call-start = ((), (), s32[]{:S(2)}) async-start(), calls=%async_computation.8 | async-start | bytes 3932160 | tf_op jit(solution)/shard_map/all_gather | solution.py:103
  7.5 6.6 %collective-permute-start = (bf16[1,3,15,512]{3,2,1,0:T(8,128)(2,1)S(1)}, bf16[1,3,15,512]{3,2,1,0:T(8,128)(2,1)S(1)}, u32[]{:S(2)}, u32[]{:S(2)}) collective-permute-start(bf16[1,3,15,512]{3,2,1,0:T(8,128)(2,1)S(1)} %slice.12), channel_id=1, source_target_pairs={{0,1},{2,3},{4,5},{6,7},{8,9},{10,11},{12,13},{14,15},{16,17},{18,... | collective-permute-start | bytes 138248 | tf_op jit(solution)/shard_map/ppermute | solution.py:12
  18.8 21.0 %copy-start.6 = (bf16[3,3,3,64]{3,2,1,0:T(4,128)(2,1)S(1)}, bf16[3,3,3,64]{3,2,1,0:T(4,128)(2,1)}, u32[]{:S(2)}) copy-start(bf16[3,3,3,64]{3,2,1,0:T(4,128)(2,1)} %param.17) | copy-start | bytes 10372
  18.8 21.0 %copy-start.8 = (pred[8,33]{0,1:T(8,128)(4,1)S(1)}, pred[8,33]{0,1:T(8,128)(4,1)}, u32[]{:S(2)}) copy-start(pred[8,33]{0,1:T(8,128)(4,1)} %constant.128) | copy-start | bytes 796
  92.3 16.8 %copy-start.5 = (bf16[3,3,64,128]{3,2,1,0:T(8,128)(2,1)S(1)}, bf16[3,3,64,128]{3,2,1,0:T(8,128)(2,1)}, u32[]{:S(2)}) copy-start(bf16[3,3,64,128]{3,2,1,0:T(8,128)(2,1)} %param.18) | copy-start | bytes 442372
  109.1 6.7 %copy-start.4 = (bf16[3,3,128,256]{3,2,1,0:T(8,128)(2,1)S(1)}, bf16[3,3,128,256]{3,2,1,0:T(8,128)(2,1)}, u32[]{:S(2)}) copy-start(bf16[3,3,128,256]{3,2,1,0:T(8,128)(2,1)} %param.19) | copy-start | bytes 1769476
  123.0 97.6 %all-gather.9.cloned.1.call-start = ((), (), s32[]{:S(2)}) async-start(), calls=%async_computation.2 | async-start | bytes 5222400 | tf_op jit(solution)/shard_map/all_gather | solution.py:93
  123.7 165.7 %all-gather.11.cloned.1.call-start = ((), (), s32[]{:S(2)}) async-start(), calls=%async_computation.3 | async-start | bytes 1740800 | tf_op jit(solution)/shard_map/all_gather | solution.py:94
  124.5 207.1 %reduce-scatter.3.cloned.1.call-start = ((), (), s32[]{:S(2)}) async-start(), calls=%async_computation.4 | async-start | bytes 3932160 | tf_op jit(solution)/shard_map/reduce_scatter | solution.py:113
  169.0 59.8 %copy-start.7 = (f32[1280]{0:T(1024)S(1)}, f32[1280]{0:T(1024)}, u32[]{:S(2)}) copy-start(f32[1280]{0:T(1024)} %param.22) | copy-start | bytes 15364
  294.9 39.9 %copy-start.3 = (f32[1280]{0:T(1024)S(1)}, f32[1280]{0:T(1024)}, u32[]{:S(2)}) copy-start(f32[1280]{0:T(1024)} %param.25) | copy-start | bytes 15364
  295.0 101.6 %all-gather.13.cloned.1.call-start = ((), (), s32[]{:S(2)}) async-start(), calls=%async_computation.5 | async-start | bytes 6963200 | tf_op jit(solution)/shard_map/all_gather | solution.py:138
  295.5 164.8 %all-gather.15.cloned.1.call-start = ((), (), s32[]{:S(2)}) async-start(), calls=%async_computation.6 | async-start | bytes 6963200 | tf_op jit(solution)/shard_map/all_gather | solution.py:142
  296.1 203.5 %all-gather.19.cloned.1.call-start = ((), (), s32[]{:S(2)}) async-start(), calls=%async_computation.9 | async-start | bytes 3932160 | tf_op jit(solution)/shard_map/all_gather | solution.py:131
  333.7 1.1 copy-start.2
  336.3 240.1 %reduce-scatter.5.cloned.1.call-start = ((), (), s32[]{:S(2)}) async-start(), calls=%async_computation.7 | async-start | bytes 3932160 | tf_op jit(solution)/shard_map/reduce_scatter | solution.py:144
  499.6 79.8 %copy-start.1 = (bf16[3,3,256,512]{3,2,1,0:T(8,128)(2,1)S(1)}, bf16[3,3,256,512]{3,2,1,0:T(8,128)(2,1)}, u32[]{:S(2)}) copy-start(bf16[3,3,256,512]{3,2,1,0:T(8,128)(2,1)} %param.20) | copy-start | bytes 7077892
Sparse Core Ops, SparseCore 0:
  123.1 41.0 all-gather.16
  166.4 54.1 all-gather.8
  222.8 38.4 all-gather.10
  295.1 36.4 reduce-scatter.2
  333.7 62.8 all-gather.12
  398.7 61.5 all-gather.14
  461.9 37.7 all-gather.18
  538.7 37.6 reduce-scatter.4
where the time goes:
time: 598 us; the launch traced here: 587 us
  waiting for transfers between devices  332 us (56%)
  matrix products  130 us (22%)
  local copies, waits for them, and re-layouts  86.5 us (14%)
  other arithmetic  19.2 us (3%)
  between operations  14.1 us (2%)
    all_gather x1, waiting for transfers between devices, on_device(): down_part = lax.all_gather(down_weight, 'dp', axis=1, tiled=True)  63.7 us
    all_gather x1, waiting for transfers between devices, on_device(): lax.all_gather(up_weight, 'dp', axis=0, tiled=True)  60.2 us
    all_gather x1, waiting for transfers between devices, on_device(): lax.all_gather(qkv_weight, 'dp', axis=0, tiled=True)  51.6 us
    dot_general x2, matrix products, device_rows(): return jnp.dot(slab, weight, preferred_element_type=jnp.float32)  44.5 us
    convert_element_type x7, local copies, waits for them, and re-layouts, conv_rows(): return jax.nn.relu(out).astype(jnp.bfloat16)  41.8 us
    all_gather x1, waiting for transfers between devices, on_device(): lax.all_gather(tokens, 'space', axis=1, tiled=True)  39.7 us
    all_gather x1, waiting for transfers between devices, on_device(): group_rows = lax.all_gather(normed_two, 'space', axis=1, tiled=True)  39.3 us
    reduce_scatter x1, waiting for transfers between devices, on_device(): lax.psum_scatter(device_rows(hidden, jnp.int32(0), groups * count * lax.a...  37.8 us
  transfers between devices with their start and end apart: 9, of which 8 were waited for; matrix products, arithmetic and copies ran while one was open for 13% of the time, Pallas kernels for 0%

commit v1 on v0

--- a/solution.py
+++ b/solution.py
@@ -139,7 +139,11 @@
         preferred_element_type=jnp.float32,
     )
     hidden = jax.nn.gelu(before_gelu, approximate=False).astype(jnp.bfloat16)
-    down_part = lax.all_gather(down_weight, "dp", axis=1, tiled=True)
+
+    def put_files_over_axis(z_in, row_dim):
+        return jnp.concatenate(jax.lax.all_gather(z_in, axis_name="dp"), axis=row_dim)
+
+    down_part = put_files_over_axis(down_weight, 1)
     mlp_sum = (
         lax.psum_scatter(
             device_rows(

time: 598 us -> 598 us (level)
  waiting for transfers between devices: 332 us -> 321 us
  local copies, waits for them, and re-layouts: 86.5 us -> 97.4 us
    all_gather x1, waiting for transfers between devices: 60.2 us -> 52.3 us  [on_device(): lax.all_gather(up_weight, 'dp', axis=0, tiled=True)]
    reshape x0 -> x1, local copies, waits for them, and re-layouts: none -> 6.34 us  [put_files_over_axis(): jnp.concatenate(jax.lax.all_gather(z_in, axis_name='dp'), axis=row_dim)]
  transfers between devices with their start and end apart: 9 -> 9, of which waited for: 8 -> 8; matrix products, arithmetic and copies ran while one was open for 13% -> 15% of each run, Pallas kernels for 0% -> 0%
where the time goes in v1:
time: 598 us; the launch traced here: 586 us
  waiting for transfers between devices  321 us (54%)
  matrix products  130 us (22%)
  local copies, waits for them, and re-layouts  97.4 us (16%)
  other arithmetic  19.2 us (3%)
  between operations  13.9 us (2%)
    all_gather x1, waiting for transfers between devices, put_files_over_axis(): jax.lax.all_gather(z_in, axis_name='dp')  60.4 us
    all_gather x1, waiting for transfers between devices, on_device(): lax.all_gather(up_weight, 'dp', axis=0, tiled=True)  52.3 us
    all_gather x1, waiting for transfers between devices, on_device(): lax.all_gather(qkv_weight, 'dp', axis=0, tiled=True)  51.6 us
    dot_general x2, matrix products, device_rows(): return jnp.dot(slab, weight, preferred_element_type=jnp.float32)  44.4 us
    convert_element_type x7, local copies, waits for them, and re-layouts, conv_rows(): return jax.nn.relu(out).astype(jnp.bfloat16)  41.8 us
    all_gather x1, waiting for transfers between devices, on_device(): lax.all_gather(tokens, 'space', axis=1, tiled=True)  39.7 us
    all_gather x1, waiting for transfers between devices, on_device(): group_rows = lax.all_gather(normed_two, 'space', axis=1, tiled=True)  39.3 us
    reduce_scatter x1, waiting for transfers between devices, on_device(): lax.psum_scatter(device_rows(hidden, jnp.int32(0), groups * count * lax.a...  37.8 us
  transfers between devices with their start and end apart: 9, of which 8 were waited for; matrix products, arithmetic and copies ran while one was open for 15% of the time, Pallas kernels for 0%

profile of v1, /device:TPU:0, one launch (start us, length us, event | category | flops | bytes accessed | tf_op | source)
XLA Modules:
  0.0 586.4 jit_solution(17830287785673419937)
XLA Ops:
  6.5 1.0 slice.12
  7.5 4.9 collective-permute-start
  12.4 1.7 collective-permute-done
  14.1 1.3 maximum_bitcast_fusion
  15.9 2.9 reshape.237
  18.8 19.6 %copy.61 = bf16[3,271,1,8,66]{3,0,4,1,2:T(4,128)(2,1)} copy(bf16[3,271,1,8,66]{4,3,1,0,2:T(8,128)(2,1)} %reshape.237) | data formatting | bytes 1717056 | tf_op jit(solution)/shard_map/conv_general_dilated | solution.py:16
  38.3 1.4 slice.25
  39.8 27.8 %fusion.44 = bf16[135,8,33,64]{3,1,2,0:T(8,128)(2,1)} fusion(pred[8,33]{0,1:T(8,128)(4,1)S(1)} %copy-done.8, bf16[3,3,3,64]{3,2,1,0:T(4,128)(2,1)S(1)} %copy-done.6, bf16[3,271,1,7,2]{3,0,4,1,2:T(4,128)(2,1)S(1)} %slice.25, bf16[3,271,1,8,66]{3,0,4,1,2:T(4,128)(2,1)} %copy.61), kind=kOutput, calls=%fused_computation.57 | convolution fusion | flops 134949312 | bytes 5446932 | tf_op jit(solution)/shard_map/conv_general_dilated | solution.py:16
  67.6 16.3 %copy.62 = bf16[135,8,33,64]{0,3,2,1:T(8,128)(2,1)} copy(bf16[135,8,33,64]{3,1,2,0:T(8,128)(2,1)} %fusion.44) | data formatting | bytes 9123840 | tf_op jit(solution)/shard_map/convert_element_type | solution.py:24
  84.0 8.3 %slice.26 = bf16[135,1,256,64]{0,3,2,1:T(8,128)(2,1)} slice(bf16[135,1,264,64]{0,3,2,1:T(8,128)(2,1)} %bitcast.129), slice={[0:135], [0:1], [0:256], [0:64]} | slice | bytes 8847360 | tf_op jit(solution)/shard_map/convert_element_type | solution.py:24
  92.3 15.6 %copy.63 = bf16[135,1,8,32,64]{4,2,3,0,1:T(8,128)(2,1)} copy(bf16[135,1,8,32,64]{0,4,3,2,1:T(8,128)(2,1)} %bitcast.130) | data formatting | bytes 8847360 | tf_op jit(solution)/shard_map/convert_element_type | solution.py:24
  107.9 1.1 fusion.155
  109.1 6.6 %fusion.86 = bf16[67,1,8,16,128]{4,2,3,0,1:T(8,128)(2,1)S(1)} fusion(bf16[3,3,64,128]{3,2,1,0:T(8,128)(2,1)S(1)} %copy-done.5, bf16[135,1,7,1,64]{4,2,3,0,1:T(8,128)(2,1)S(1)} %get-tuple-element.68, bf16[135,1,7,1,64]{4,2,3,0,1:T(8,128)(2,1)S(1)} %get-tuple-element.67, bf16[135,1,8,32,64]{4,2,3,0,1:T(8,128)(2,1)} %copy.63), kind=kOutput, calls=%fused_computation.105 | convolution fusion | flops 1290278912 | bytes 7008512 | tf_op jit(solution)/shard_map/conv_general_dilated | solution.py:16
  115.8 1.6 fusion.91
  117.5 1.4 fusion.105
  119.3 3.7 fusion.63
  123.0 0.7 all-gather.10.cloned.1.call-update
  123.8 0.7 all-gather.12.cloned.1.call-update
  124.5 39.7 %all-gather.16.cloned.1.call-done = bf16[1024,1280]{1,0:T(8,128)(2,1)} async-done(((bf16[512,1280]{1,0:T(8,128)(2,1)}), bf16[1024,1280]{1,0:T(8,128)(2,1)}) %all-gather.16.cloned.1.call-update) | async-done | bytes 2621456 | tf_op jit(solution)/shard_map/all_gather | solution.py:103
  164.2 2.1 convert_reduce_fusion
  166.4 2.6 fusion.50
  169.0 51.6 %all-gather.10.cloned.1.call-done = bf16[1280,3,640]{2,0,1:T(8,128)(2,1)} async-done(((bf16[80,3,640]{2,0,1:T(8,128)(2,1)}), bf16[1280,3,640]{2,0,1:T(8,128)(2,1)}) %all-gather.10.cloned.1.call-update) | async-done | bytes 4915216 | tf_op jit(solution)/shard_map/all_gather | solution.py:93
  220.6 8.2 %copy.67 = bf16[1280,3,640]{0,2,1:T(8,128)(2,1)} copy(bf16[1280,3,640]{2,0,1:T(8,128)(2,1)} %all-gather.10.cloned.1.call-done) | data formatting | bytes 9830400 | tf_op jit(solution)/shard_map/all_gather | solution.py:93
  228.8 10.3 %convolution_convert_fusion.1 = bf16[1024,1920]{1,0:T(8,128)(2,1)} fusion(bf16[1280,1920]{0,1:T(8,128)(2,1)} %bitcast.135, bf16[1024,1280]{1,0:T(8,128)(2,1)} %all-gather.16.cloned.1.call-done, f32[1280]{0:T(1024)S(1)} %copy-done.7, f32[1024]{0:T(1024)S(1)} %add_rsqrt_fusion, f32[1024]{0:T(1024)S(1)} %broadcast_multiply_fusion), kind=kOutput, calls=%fused_computation.78 | convolution fusion | flops 5041684480 | bytes 11482112 | tf_op jit(solution)/shard_map/dot_general | solution.py:102
  239.0 6.3 %copy.68 = bf16[1024,1920]{0,1:T(8,128)(2,1)} copy(bf16[1024,1920]{1,0:T(8,128)(2,1)} %convolution_convert_fusion.1) | data formatting | bytes 7864320 | tf_op jit(solution)/shard_map/convert_element_type | solution.py:106
  245.3 4.2 slice_bitcast_fusion
  249.5 39.8 %while.10 = (s32[]{:T(128)}, bf16[8,1,1024,80]{2,3,1,0:T(8,128)(2,1)}, bf16[8,1,1024,80]{2,3,0,1:T(8,128)(2,1)}, bf16[8,1,1024,80]{2,3,0,1:T(8,128)(2,1)S(1)}, bf16[8,1,1024,80]{2,3,0,1:T(8,128)(2,1)}, /*index=5*/s32[]{:T(128)}) while((s32[]{:T(128)}, bf16[8,1,1024,80]{2,3,1,0:T(8,128)(2,1)}, bf16[8,1,1024,80]{2,3,0,1:T(8,128)(2,1)}, ...), condition=%wide.region_5.6_spmd, body=%wide.region_2.5_spmd.sunk | while | flops 345061376 | bytes 13260869 | solution.py:49
  249.5 1.7 multiply_reduce_fusion.2
  251.2 0.7 fusion.186
  252.0 2.6 fusion.187
  254.5 1.7 multiply_reduce_fusion.2
  256.2 0.7 fusion.186
  256.9 2.6 fusion.187
  259.5 1.7 multiply_reduce_fusion.2
  261.2 0.7 fusion.186
  261.9 2.6 fusion.187
  264.5 1.7 multiply_reduce_fusion.2
  266.2 0.7 fusion.186
  266.9 2.6 fusion.187
  269.5 1.7 multiply_reduce_fusion.2
  271.1 0.7 fusion.186
  271.9 2.6 fusion.187
  274.4 1.7 multiply_reduce_fusion.2
  276.1 0.7 fusion.186
  276.9 2.6 fusion.187
  279.4 1.7 multiply_reduce_fusion.2
  281.1 0.7 fusion.186
  281.8 2.6 fusion.187
  284.4 1.7 multiply_reduce_fusion.2
  286.1 0.7 fusion.186
  286.8 2.6 fusion.187
  289.4 5.5 convolution_convert_fusion
  295.0 0.5 all-gather.20.cloned.1.call-update
  296.2 35.4 %reduce-scatter.3.cloned.1.call-done = bf16[512,1280]{1,0:T(8,128)(2,1)} async-done(((bf16[1024,1280]{1,0:T(8,128)(2,1)}), bf16[512,1280]{1,0:T(8,128)(2,1)}) %reduce-scatter.3.cloned.1.call-update) | async-done | bytes 1310736 | tf_op jit(solution)/shard_map/reduce_scatter | solution.py:113
  331.5 2.2 convert_reduce_fusion.1
  334.2 1.5 fusion.68
  336.2 60.4 %all-gather.20.cloned.1.call-done = bf16[40960,80]{0,1:T(8,128)(2,1)} async-done(((bf16[2560,80]{0,1:T(8,128)(2,1)}), bf16[40960,80]{0,1:T(8,128)(2,1)}) %all-gather.20.cloned.1.call-update) | async-done | bytes 6553616 | tf_op jit(solution)/shard_map/all_gather | solution.py:144
  396.6 5.1 copy.78
  401.7 6.3 %copy.72 = bf16[2560,16,80]{0,2,1:T(8,128)(2,1)} copy(bf16[2560,16,80]{0,1,2:T(8,128)(2,1)S(1)} %bitcast.131) | data formatting | bytes 13107200 | tf_op jit(solution)/shard_map/reshape | solution.py:144
  408.1 52.3 %all-gather.14.cloned.1.call-done = bf16[1280,2560]{1,0:T(8,128)(2,1)} async-done(((bf16[80,2560]{1,0:T(8,128)(2,1)}), bf16[1280,2560]{1,0:T(8,128)(2,1)}) %all-gather.14.cloned.1.call-update) | async-done | bytes 6553616 | tf_op jit(solution)/shard_map/all_gather | solution.py:138
  460.3 39.3 %all-gather.18.cloned.1.call-done = bf16[1024,1280]{1,0:T(8,128)(2,1)} async-done(((bf16[512,1280]{1,0:T(8,128)(2,1)}), bf16[1024,1280]{1,0:T(8,128)(2,1)}) %all-gather.18.cloned.1.call-update) | async-done | bytes 2621456 | tf_op jit(solution)/shard_map/all_gather | solution.py:131
  499.6 38.9 %fusion.58 = bf16[1024,1280]{1,0:T(8,128)(2,1)} fusion(bf16[2560,1280]{0,1:T(8,128)(2,1)} %bitcast.134, bf16[1024,1280]{1,0:T(8,128)(2,1)} %all-gather.18.cloned.1.call-done, bf16[1280,2560]{1,0:T(8,128)(2,1)} %all-gather.14.cloned.1.call-done), kind=kOutput, calls=%fused_computation.76 | convolution fusion | flops 13593477120 | bytes 18350080 | tf_op jit(solution)/shard_map/dot_general | solution.py:62
  538.5 37.8 %reduce-scatter.5.cloned.1.call-done = bf16[512,1280]{1,0:T(8,128)(2,1)} async-done(((bf16[1024,1280]{1,0:T(8,128)(2,1)}), bf16[512,1280]{1,0:T(8,128)(2,1)}) %reduce-scatter.5.cloned.1.call-update) | async-done | bytes 1310736 | tf_op jit(solution)/shard_map/reduce_scatter | solution.py:148
  576.3 3.1 fusion.104
  (43 shorter events, 2.8 us)
Async XLA Ops:
  6.5 110.9 %copy-start = (bf16[3,3,256,512]{3,2,1,0:T(8,128)(2,1)S(1)}, bf16[3,3,256,512]{3,2,1,0:T(8,128)(2,1)}, u32[]{:S(2)}) copy-start(bf16[3,3,256,512]{3,2,1,0:T(8,128)(2,1)} %param.20) | copy-start | bytes 7077892
  6.5 157.7 %all-gather.16.cloned.1.call-start = ((), (), s32[]{:S(2)}) async-start(), calls=%async_computation.7 | async-start | bytes 3932160 | tf_op jit(solution)/shard_map/all_gather | solution.py:103
  7.5 6.6 %collective-permute-start = (bf16[1,3,15,512]{3,2,1,0:T(8,128)(2,1)S(1)}, bf16[1,3,15,512]{3,2,1,0:T(8,128)(2,1)S(1)}, u32[]{:S(2)}, u32[]{:S(2)}) collective-permute-start(bf16[1,3,15,512]{3,2,1,0:T(8,128)(2,1)S(1)} %slice.12), channel_id=1, source_target_pairs={{0,1},{2,3},{4,5},{6,7},{8,9},{10,11},{12,13},{14,15},{16,17},{18,... | collective-permute-start | bytes 138248 | tf_op jit(solution)/shard_map/ppermute | solution.py:12
  18.8 21.0 %copy-start.6 = (bf16[3,3,3,64]{3,2,1,0:T(4,128)(2,1)S(1)}, bf16[3,3,3,64]{3,2,1,0:T(4,128)(2,1)}, u32[]{:S(2)}) copy-start(bf16[3,3,3,64]{3,2,1,0:T(4,128)(2,1)} %param.17) | copy-start | bytes 10372
  18.8 21.0 %copy-start.8 = (pred[8,33]{0,1:T(8,128)(4,1)S(1)}, pred[8,33]{0,1:T(8,128)(4,1)}, u32[]{:S(2)}) copy-start(pred[8,33]{0,1:T(8,128)(4,1)} %constant.128) | copy-start | bytes 796
  92.3 16.8 %copy-start.5 = (bf16[3,3,64,128]{3,2,1,0:T(8,128)(2,1)S(1)}, bf16[3,3,64,128]{3,2,1,0:T(8,128)(2,1)}, u32[]{:S(2)}) copy-start(bf16[3,3,64,128]{3,2,1,0:T(8,128)(2,1)} %param.18) | copy-start | bytes 442372
  109.1 6.7 %copy-start.4 = (bf16[3,3,128,256]{3,2,1,0:T(8,128)(2,1)S(1)}, bf16[3,3,128,256]{3,2,1,0:T(8,128)(2,1)}, u32[]{:S(2)}) copy-start(bf16[3,3,128,256]{3,2,1,0:T(8,128)(2,1)} %param.19) | copy-start | bytes 1769476
  123.0 97.6 %all-gather.10.cloned.1.call-start = ((), (), s32[]{:S(2)}) async-start(), calls=%async_computation.2 | async-start | bytes 5222400 | tf_op jit(solution)/shard_map/all_gather | solution.py:93
  123.7 165.6 %all-gather.12.cloned.1.call-start = ((), (), s32[]{:S(2)}) async-start(), calls=%async_computation.3 | async-start | bytes 1740800 | tf_op jit(solution)/shard_map/all_gather | solution.py:94
  124.5 207.1 %reduce-scatter.3.cloned.1.call-start = ((), (), s32[]{:S(2)}) async-start(), calls=%async_computation.4 | async-start | bytes 3932160 | tf_op jit(solution)/shard_map/reduce_scatter | solution.py:113
  168.9 59.8 %copy-start.7 = (f32[1280]{0:T(1024)S(1)}, f32[1280]{0:T(1024)}, u32[]{:S(2)}) copy-start(f32[1280]{0:T(1024)} %param.22) | copy-start | bytes 15364
  294.9 39.3 %copy-start.3 = (f32[1280]{0:T(1024)S(1)}, f32[1280]{0:T(1024)}, u32[]{:S(2)}) copy-start(f32[1280]{0:T(1024)} %param.25) | copy-start | bytes 15364
  295.0 101.6 %all-gather.20.cloned.1.call-start = ((), (), s32[]{:S(2)}) async-start(), calls=%async_computation.9 | async-start | bytes 6963200 | tf_op jit(solution)/shard_map/all_gather | solution.py:144
  295.5 164.8 %all-gather.14.cloned.1.call-start = ((), (), s32[]{:S(2)}) async-start(), calls=%async_computation.5 | async-start | bytes 6963200 | tf_op jit(solution)/shard_map/all_gather | solution.py:138
  296.1 203.5 %all-gather.18.cloned.1.call-start = ((), (), s32[]{:S(2)}) async-start(), calls=%async_computation.8 | async-start | bytes 3932160 | tf_op jit(solution)/shard_map/all_gather | solution.py:131
  333.7 68.0 %copy-start.2 = (bf16[512,1280]{1,0:T(8,128)(2,1)}, bf16[512,1280]{1,0:T(8,128)(2,1)S(1)}, u32[]{:S(2)}) copy-start(bf16[512,1280]{1,0:T(8,128)(2,1)S(1)} %get-tuple-element.64) | copy-start | bytes 3932164
  335.8 240.6 %reduce-scatter.5.cloned.1.call-start = ((), (), s32[]{:S(2)}) async-start(), calls=%async_computation.6 | async-start | bytes 3932160 | tf_op jit(solution)/shard_map/reduce_scatter | solution.py:148
  499.6 79.8 %copy-start.1 = (bf16[3,3,256,512]{3,2,1,0:T(8,128)(2,1)S(1)}, bf16[3,3,256,512]{3,2,1,0:T(8,128)(2,1)}, u32[]{:S(2)}) copy-start(bf16[3,3,256,512]{3,2,1,0:T(8,128)(2,1)} %param.20) | copy-start | bytes 7077892
Sparse Core Ops, SparseCore 0:
  123.1 41.0 all-gather.15
  166.4 54.1 all-gather.9
  222.8 38.4 all-gather.11
  295.1 36.4 reduce-scatter.2
  333.7 62.8 all-gather.19
  398.7 61.5 all-gather.13
  461.9 37.7 all-gather.17
  538.6 37.6 reduce-scatter.4
